TPU v7x, 32 devices: a whole 2x2x4 slice. The times are simulated.
32 devices in a mesh: tm: 4 (over z), ent: 2 (over y), batch: 4 (over x, core).
Axes of the slice: x: 2, y: 2, z: 4, core: 2. Of those that a mesh axis runs over, the one named last changes fastest.
Arguments:
- init_state: float32 [4, 1024, 256], P('batch', 'ent'), may hold values from -6 to 6
- tiles: float32 [4, 4, 4, 512, 512], P('batch', 'tm', 'ent'), may hold values from -0.25 to 0.25
- dst_block: int32 [4, 4, 4], P('batch', 'tm', 'ent'), may hold values from 0 to 1
- rel_id: int32 [4, 4, 4], P('batch', 'tm', 'ent'), may hold values from 0 to 255
- cotangent: float32 [4, 4, 1024, 256], P('batch', 'tm', 'ent'), may hold values from -0.125 to 0.125
- rel_emb: float32 [256, 256], replicated, may hold values from -6 to 6
- w_neigh: float32 [256, 256], replicated, may hold values from -0.1875 to 0.1875
- w_self: float32 [256, 256], replicated, may hold values from -0.375 to 0.375
- w_gate: float32 [256, 256], replicated, may hold values from -0.375 to 0.375
- b_gate: float32 [256], replicated, may hold values from -2 to 2
Outputs:
- states: float32 [4, 4, 1024, 256], P('batch', 'tm', 'ent')
- grad_rel: float32 [256, 256], replicated
- grad_neigh: float32 [256, 256], replicated
- grad_self: float32 [256, 256], replicated
- grad_gate: float32 [256, 256], replicated
- grad_bias: float32 [256], replicated
All inputs are finite; a program needn't handle non-finite values.
Results may differ from a plain program's by a relative error of at most 0.00012.
Values sent between devices are 32-bit elements; how exact they have to be, the bound alone decides.
A program may use at most 64 MiB of HBM per device.

v0:
```python
import jax
import jax.numpy as jnp
from jax import lax
from jax.sharding import PartitionSpec as P

highest = lax.Precision.HIGHEST


def shifted(value, axis, steps):
    count = lax.axis_size(axis)
    first, last = (max(0, -steps), min(count, count - steps))
    return lax.ppermute(value, axis, [(source, source + steps) for source in range(first, last)])


def product(left, right):
    return jnp.dot(left, right, precision=highest)


def block_terms(current, tiles_t, rel_t, rel_emb):
    rows_sum = jnp.sum(tiles_t, axis=2)
    rel_pick = (rel_t[:, None] == jnp.arange(rel_emb.shape[0], dtype=jnp.int32)[None, :]).astype(
        jnp.float32
    )
    rel_rows = product(rel_pick, rel_emb)
    result = jnp.einsum("tij,jd->tid", tiles_t, current, precision=highest)
    return result + rows_sum[:, :, None] * rel_rows[:, None, :]


def dest_table(dst_t):
    count = lax.axis_size("ent")
    return (dst_t[:, None] == jnp.arange(count, dtype=jnp.int32)[None, :]).astype(jnp.float32)


def gru_forward(current, incoming, params):
    rel_emb, w_neigh, w_self, w_gate, b_gate = params
    update_gate = jax.nn.sigmoid(product(current, w_gate) + b_gate)
    candidate = jnp.tanh(product(incoming, w_neigh) + product(current, w_self))
    return (update_gate * candidate + (1.0 - update_gate) * current, update_gate, candidate)


def gru_backward(d_new, current, incoming, update_gate, candidate, params):
    rel_emb, w_neigh, w_self, w_gate, b_gate = params
    d_update = d_new * (candidate - current)
    d_cand = d_new * update_gate
    d_pre = d_cand * (1.0 - candidate * candidate)
    d_gate_in = d_update * update_gate * (1.0 - update_gate)
    d_prev = d_new * (1.0 - update_gate) + product(d_pre, w_self.T) + product(d_gate_in, w_gate.T)
    d_incoming = product(d_pre, w_neigh.T)
    dense_grads = (
        product(incoming.T, d_pre),
        product(current.T, d_pre),
        product(current.T, d_gate_in),
        jnp.sum(d_gate_in, axis=0),
    )
    return (d_prev, d_incoming, dense_grads)


def tile_backward(d_res, tiles_t, rel_t, rel_count):
    d_held = jnp.einsum("tij,tid->jd", tiles_t, d_res, precision=highest)
    rows_sum = jnp.sum(tiles_t, axis=2)
    per_tile = jnp.einsum("ti,tid->td", rows_sum, d_res, precision=highest)
    rel_pick = (rel_t[:, None] == jnp.arange(rel_count, dtype=jnp.int32)[None, :]).astype(
        jnp.float32
    )
    return (d_held, jnp.einsum("tr,td->rd", rel_pick, per_tile, precision=highest))


def natural_step(current, tiles_t, dst_t, rel_t, params):
    result = block_terms(current, tiles_t, rel_t, params[0])
    partial_value = jnp.einsum("tg,tid->gid", dest_table(dst_t), result, precision=highest)
    incoming = lax.psum_scatter(partial_value, "ent", scatter_dimension=0, tiled=True)[0]
    return (incoming,) + gru_forward(current, incoming, params)


def natural_spread(d_incoming, dst_t):
    gathered = lax.all_gather(d_incoming[None], "ent", axis=0, tiled=True)
    return jnp.einsum("tg,gid->tid", dest_table(dst_t), gathered, precision=highest)


def run_forward(begin_state, stacks, params, advance_fn):

    def advance(current, inputs):
        tiles_t, dst_t, rel_t = inputs
        incoming, new_state, update_gate, candidate = advance_fn(
            current, tiles_t, dst_t, rel_t, params
        )
        return (new_state, (current, incoming, update_gate, candidate, new_state))

    return lax.scan(advance, begin_state, stacks)


def run_backward(d_last, stored, stacks, targets, params, spread_fn):
    rel_emb = params[0]
    empty = (
        jnp.zeros_like(rel_emb),
        jnp.zeros_like(params[1]),
        jnp.zeros_like(params[2]),
        jnp.zeros_like(params[3]),
        jnp.zeros_like(params[4]),
    )

    def retreat(carry, inputs):
        d_state, weight_sums = carry
        (current, incoming, update_gate, candidate), (tiles_t, dst_t, rel_t), target_t = inputs
        d_new = d_state + target_t
        d_prev, d_incoming, dense_grads = gru_backward(
            d_new, current, incoming, update_gate, candidate, params
        )
        d_res = spread_fn(d_incoming, dst_t)
        d_held, d_rel = tile_backward(d_res, tiles_t, rel_t, rel_emb.shape[0])
        summed = (
            weight_sums[0] + d_rel,
            weight_sums[1] + dense_grads[0],
            weight_sums[2] + dense_grads[1],
            weight_sums[3] + dense_grads[2],
            weight_sums[4] + dense_grads[3],
        )
        return ((d_prev + d_held, summed), None)

    (d_first, weight_sums), unused = lax.scan(
        retreat, (d_last, empty), (stored, stacks, targets), reverse=True
    )
    return (d_first, weight_sums)


def on_device(
    init_state, tiles, dst_block, rel_id, cotangent, rel_emb, w_neigh, w_self, w_gate, b_gate
):
    params = (rel_emb, w_neigh, w_self, w_gate, b_gate)
    n_tm = lax.axis_size("tm")
    stacks = (tiles[0], dst_block[0], rel_id[0])
    targets = cotangent[0]
    is_first = lax.axis_index("tm") == 0
    begin_state = init_state[0]
    stored_all = None
    for round_index in range(n_tm):
        last_state, stored_all = run_forward(begin_state, stacks, params, natural_step)
        if round_index + 1 < n_tm:
            passed = shifted(last_state, "tm", 1)
            begin_state = jnp.where(is_first, init_state[0], passed)
    stored = stored_all[:4]
    d_last = jnp.zeros_like(init_state[0])
    weight_grads = None
    for round_index in range(n_tm):
        d_first, weight_grads = run_backward(
            d_last, stored, stacks, targets, params, natural_spread
        )
        if round_index + 1 < n_tm:
            d_last = shifted(d_first, "tm", -1)
    state_out = stored_all[4][None]
    totals = lax.psum(weight_grads, ("tm", "ent", "batch"))
    return (state_out, totals[0], totals[1], totals[2], totals[3], totals[4])


def solution(mesh):
    placed = (
        P("batch", "ent", None),
        P("batch", "tm", "ent", None, None),
        P("batch", "tm", "ent"),
        P("batch", "tm", "ent"),
        P("batch", "tm", "ent", None),
        P(),
        P(),
        P(),
        P(),
        P(),
    )
    return jax.shard_map(
        on_device,
        mesh=mesh,
        in_specs=placed,
        out_specs=(P("batch", "tm", "ent", None), P(), P(), P(), P(), P()),
        check_vma=False,
    )
```

profile of v0, /device:TPU:13, one launch (start us, length us, event | category | flops | bytes accessed | tf_op | source)
XLA Modules:
  0.0 517.4 jit_solution(6965761714206291700)
XLA Ops:
  7.2 2.0 reduce_sum.32
  9.4 2.9 fusion.12
  12.6 3.5 fusion.66
  18.9 18.9 %reduce-scatter.5.cloned.1.call-done = f32[1,512,256]{2,1,0:T(8,128)} async-done(((f32[2,512,256]{2,1,0:T(8,128)}), f32[1,512,256]{2,1,0:T(8,128)}) %reduce-scatter.5.cloned.1.call-update) | async-done | bytes 524304 | tf_op jit(solution)/shard_map/while/body/eval_jaxpr/reduce_scatter | solution.py:71
  37.9 1.6 fusion.82
  39.5 2.5 fusion.45
  42.0 3.3 collective-permute-start
  45.3 11.6 %collective-permute-done = f32[512,256]{1,0:T(8,128)} collective-permute-done((f32[512,256]{1,0:T(8,128)}, f32[512,256]{1,0:T(8,128)}, u32[]{:S(2)}, u32[]{:S(2)}) %collective-permute-start) | collective-permute-done | bytes 524320 | tf_op jit(solution)/shard_map/ppermute | solution.py:12
  58.7 4.5 fusion.10
  63.2 2.2 copy.28
  65.5 3.8 fusion.63
  70.4 2.4 fusion.42
  72.9 18.9 %reduce-scatter.7.cloned.1.call-done = f32[1,512,256]{2,1,0:T(8,128)} async-done(((f32[2,512,256]{2,1,0:T(8,128)}), f32[1,512,256]{2,1,0:T(8,128)}) %reduce-scatter.7.cloned.1.call-update) | async-done | bytes 524304 | tf_op jit(solution)/shard_map/while/body/eval_jaxpr/reduce_scatter | solution.py:71
  91.7 1.6 fusion.79
  93.4 2.0 fusion.38
  95.4 3.3 collective-permute-start.1
  98.8 11.2 %collective-permute-done.1 = f32[512,256]{1,0:T(8,128)S(1)} collective-permute-done((f32[512,256]{1,0:T(8,128)S(1)}, f32[512,256]{1,0:T(8,128)S(1)}, u32[]{:S(2)}, u32[]{:S(2)}) %collective-permute-start.1) | collective-permute-done | bytes 524320 | tf_op jit(solution)/shard_map/ppermute | solution.py:12
  110.8 4.5 fusion.8
  115.3 2.2 copy.29
  117.6 3.7 fusion.64
  123.9 19.9 %reduce-scatter.9.cloned.1.call-done = f32[1,512,256]{2,1,0:T(8,128)} async-done(((f32[2,512,256]{2,1,0:T(8,128)}), f32[1,512,256]{2,1,0:T(8,128)}) %reduce-scatter.9.cloned.1.call-update) | async-done | bytes 524304 | tf_op jit(solution)/shard_map/while/body/eval_jaxpr/reduce_scatter | solution.py:71
  143.9 1.7 fusion.76
  145.6 1.6 fusion.31
  147.2 3.4 collective-permute-start.2
  150.6 11.1 %collective-permute-done.2 = f32[512,256]{1,0:T(8,128)S(1)} collective-permute-done((f32[512,256]{1,0:T(8,128)S(1)}, f32[512,256]{1,0:T(8,128)S(1)}, u32[]{:S(2)}, u32[]{:S(2)}) %collective-permute-start.2) | collective-permute-done | bytes 524320 | tf_op jit(solution)/shard_map/ppermute | solution.py:12
  161.8 4.5 fusion.6
  166.3 2.2 copy.30
  168.6 3.7 fusion.65
  173.5 1.6 fusion.28
  175.1 19.8 %reduce-scatter.11.cloned.1.call-done = f32[1,512,256]{2,1,0:T(8,128)} async-done(((f32[2,512,256]{2,1,0:T(8,128)}), f32[1,512,256]{2,1,0:T(8,128)}) %reduce-scatter.11.cloned.1.call-update) | async-done | bytes 524304 | tf_op jit(solution)/shard_map/while/body/eval_jaxpr/reduce_scatter | solution.py:71
  194.9 1.7 fusion.73
  196.6 2.7 fusion.145
  200.1 1.4 fusion.113
  202.1 2.5 convolution_add_fusion.1
  204.5 18.5 %all-gather.9.cloned.1.call-done = f32[1024,256]{1,0:T(8,128)} async-done(((f32[512,256]{1,0:T(8,128)}), f32[1024,256]{1,0:T(8,128)}) %all-gather.9.cloned.1.call-update) | async-done | bytes 1048592 | tf_op jit(solution)/shard_map/while/body/eval_jaxpr/all_gather | solution.py:76
  223.0 4.5 fusion.61
  227.5 3.4 fusion.14
  231.7 2.3 collective-permute-start.3
  234.0 12.4 %collective-permute-done.3 = f32[512,256]{1,0:T(8,128)S(1)} collective-permute-done((f32[512,256]{1,0:T(8,128)S(1)}, f32[512,256]{1,0:T(8,128)S(1)}, u32[]{:S(2)}, u32[]{:S(2)}) %collective-permute-start.3) | collective-permute-done | bytes 524320 | tf_op jit(solution)/shard_map/ppermute | solution.py:12
  249.7 2.4 fusion.146
  252.1 18.7 %all-gather.11.cloned.1.call-done = f32[1024,256]{1,0:T(8,128)} async-done(((f32[512,256]{1,0:T(8,128)}), f32[1024,256]{1,0:T(8,128)}) %all-gather.11.cloned.1.call-update) | async-done | bytes 1048592 | tf_op jit(solution)/shard_map/while/body/eval_jaxpr/all_gather | solution.py:76
  270.8 4.5 fusion.59
  275.3 3.4 fusion.17
  279.6 2.3 collective-permute-start.4
  281.9 12.4 %collective-permute-done.4 = f32[512,256]{1,0:T(8,128)S(1)} collective-permute-done((f32[512,256]{1,0:T(8,128)S(1)}, f32[512,256]{1,0:T(8,128)S(1)}, u32[]{:S(2)}, u32[]{:S(2)}) %collective-permute-start.4) | collective-permute-done | bytes 524320 | tf_op jit(solution)/shard_map/ppermute | solution.py:12
  295.9 1.4 fusion.149
  297.6 2.4 fusion.148
  300.0 18.7 %all-gather.13.cloned.1.call-done = f32[1024,256]{1,0:T(8,128)} async-done(((f32[512,256]{1,0:T(8,128)}), f32[1024,256]{1,0:T(8,128)}) %all-gather.13.cloned.1.call-update) | async-done | bytes 1048592 | tf_op jit(solution)/shard_map/while/body/eval_jaxpr/all_gather | solution.py:76
  318.7 4.5 fusion.57
  323.2 3.5 fusion.20
  327.5 2.3 collective-permute-start.5
  329.8 12.4 %collective-permute-done.5 = f32[512,256]{1,0:T(8,128)S(1)} collective-permute-done((f32[512,256]{1,0:T(8,128)S(1)}, f32[512,256]{1,0:T(8,128)S(1)}, u32[]{:S(2)}, u32[]{:S(2)}) %collective-permute-start.5) | collective-permute-done | bytes 524320 | tf_op jit(solution)/shard_map/ppermute | solution.py:12
  343.4 1.4 fusion.150
  345.1 1.7 fusion.151
  346.8 1.7 fusion.152
  348.5 1.7 fusion.71
  350.2 15.9 %all-gather.15.cloned.1.call-done = f32[1024,256]{1,0:T(8,128)} async-done(((f32[512,256]{1,0:T(8,128)}), f32[1024,256]{1,0:T(8,128)}) %all-gather.15.cloned.1.call-update) | async-done | bytes 1048592 | tf_op jit(solution)/shard_map/while/body/eval_jaxpr/all_gather | solution.py:76
  366.2 4.5 fusion.55
  372.4 40.8 %psum.39 = f32[256]{0:T(256)} all-reduce(f32[256]{0:T(256)S(1)} %get-tuple-element.207), channel_id=1, replica_groups=mesh['tm'=4,'ent'=2,'batch'=4] {'tm','ent','batch'}, use_global_device_ids=true, to_apply=%region_10.11 | all-reduce | flops 256 | bytes 2048 | tf_op jit(solution)/shard_map/psum | solution.py:151
  413.2 90.7 %all-reduce.3.cloned.1.call-done = (f32[256,256]{1,0:T(8,128)}, f32[256,256]{1,0:T(8,128)}, f32[256,256]{1,0:T(8,128)}, f32[256,256]{1,0:T(8,128)}) async-done(((f32[256,256]{1,0:T(8,128)}, f32[256,256]{1,0:T(8,128)}, f32[256,256]{1,0:T(8,128)}, f32[256,256]{1,0:T(8,128)}), (f32[256,256]{1,0:T(8,128)}, f32[256,256]{1,0:T(8,128)}, f32[256,256]{1,0:T(8,128)}, ...) | async-done | bytes 1048592 | tf_op jit(solution)/shard_map/psum | solution.py:151
  503.9 1.7 copy.75
  505.6 1.7 copy.76
  507.2 1.7 copy.77
  508.9 1.7 copy.78
  (126 shorter events, 22.8 us)
Async XLA Ops:
  7.2 32.3 %copy-start = (f32[256,256]{1,0:T(8,128)S(1)}, f32[256,256]{1,0:T(8,128)}, u32[]{:S(2)}) copy-start(f32[256,256]{1,0:T(8,128)} %param.17) | copy-start | bytes 786436
  7.2 2.3 copy-start.1
  7.2 30.7 %reduce-scatter.5.cloned.1.call-start = ((), (), s32[]{:S(2)}) async-start(), calls=%async_computation.4 | async-start | bytes 1572864 | tf_op jit(solution)/shard_map/while/body/eval_jaxpr/reduce_scatter | solution.py:71
  9.2 3.2 copy-start.37
  9.2 3.2 copy-start.42
  9.2 3.4 copy-start.41
  9.4 3.1 copy-start.38
  16.2 1.2 copy-start.14
  16.2 1.4 copy-start.24
  16.2 1.3 copy-start.43
  17.3 20.6 %copy-start.9 = (f32[256,256]{1,0:T(8,128)S(1)}, f32[256,256]{1,0:T(8,128)}, u32[]{:S(2)}) copy-start(f32[256,256]{1,0:T(8,128)} %param.16) | copy-start | bytes 786436
  17.3 74.4 %reduce-scatter.7.cloned.1.call-start = ((), (), s32[]{:S(2)}) async-start(), calls=%async_computation.5 | async-start | bytes 1572864 | tf_op jit(solution)/shard_map/while/body/eval_jaxpr/reduce_scatter | solution.py:71
  42.0 14.8 %collective-permute-start = (f32[512,256]{1,0:T(8,128)}, f32[512,256]{1,0:T(8,128)}, u32[]{:S(2)}, u32[]{:S(2)}) collective-permute-start(f32[512,256]{1,0:T(8,128)} %fusion.45), channel_id=1, source_target_pairs={{0,8},{8,16},{16,24},{1,9},{9,17},{17,25},{2,10},{10,18},{18,26},{... | collective-permute-start | bytes 1572872 | tf_op jit(solution)/shard_map/ppermute | solution.py:12
  57.9 0.8 copy-start.21
  70.4 73.5 %reduce-scatter.9.cloned.1.call-start = ((), (), s32[]{:S(2)}) async-start(), calls=%async_computation.6 | async-start | bytes 1572864 | tf_op jit(solution)/shard_map/while/body/eval_jaxpr/reduce_scatter | solution.py:71
  95.4 14.5 %collective-permute-start.1 = (f32[512,256]{1,0:T(8,128)S(1)}, f32[512,256]{1,0:T(8,128)S(1)}, u32[]{:S(2)}, u32[]{:S(2)}) collective-permute-start(f32[512,256]{1,0:T(8,128)S(1)} %fusion.38), channel_id=1, source_target_pairs={{0,8},{8,16},{16,24},{1,9},{9,17},{17,25},{2,10},{10,18},{18,26},{... | collective-permute-start | bytes 1572872 | tf_op jit(solution)/shard_map/ppermute | solution.py:12
  110.0 0.8 copy-start.22
  110.8 6.8 %copy-start.39 = (f32[2,512]{0,1:T(8,128)S(1)}, f32[2,512]{0,1:T(8,128)}, u32[]{:S(2)}) copy-start(f32[2,512]{0,1:T(8,128)} %copy-done.38) | copy-start | bytes 12292
  121.3 1.2 copy-start.23
  122.5 72.4 %reduce-scatter.11.cloned.1.call-start = ((), (), s32[]{:S(2)}) async-start(), calls=%async_computation.7 | async-start | bytes 1572864 | tf_op jit(solution)/shard_map/while/body/eval_jaxpr/reduce_scatter | solution.py:71
  143.9 17.9 %copy-start.15 = (f32[1,512,256]{2,1,0:T(8,128)S(1)}, f32[1,512,256]{2,1,0:T(8,128)}, u32[]{:S(2)}) copy-start(f32[1,512,256]{2,1,0:T(8,128)} %param.10) | copy-start | bytes 1572868
  147.2 14.5 %collective-permute-start.2 = (f32[512,256]{1,0:T(8,128)S(1)}, f32[512,256]{1,0:T(8,128)S(1)}, u32[]{:S(2)}, u32[]{:S(2)}) collective-permute-start(f32[512,256]{1,0:T(8,128)S(1)} %fusion.31), channel_id=1, source_target_pairs={{0,8},{8,16},{16,24},{1,9},{9,17},{17,25},{2,10},{10,18},{18,26},{... | collective-permute-start | bytes 1572872 | tf_op jit(solution)/shard_map/ppermute | solution.py:12
  161.8 11.7 %copy-start.3 = (f32[512,256]{1,0:T(8,128)}, f32[512,256]{1,0:T(8,128)S(1)}, u32[]{:S(2)}) copy-start(f32[512,256]{1,0:T(8,128)S(1)} %bitcast_select_fusion.2) | copy-start | bytes 1572868
  161.8 6.8 %copy-start.40 = (f32[2,512]{0,1:T(8,128)S(1)}, f32[2,512]{0,1:T(8,128)}, u32[]{:S(2)}) copy-start(f32[2,512]{0,1:T(8,128)} %copy-done.38) | copy-start | bytes 12292
  173.4 49.6 %all-gather.9.cloned.1.call-start = ((), (), s32[]{:S(2)}) async-start(), calls=%async_computation.8 | async-start | bytes 1572864 | tf_op jit(solution)/shard_map/while/body/eval_jaxpr/all_gather | solution.py:76
  175.1 25.1 %copy-start.2 = (f32[1,1,512,256]{3,2,1,0:T(8,128)S(1)}, f32[1,1,512,256]{3,2,1,0:T(8,128)}, u32[]{:S(2)}) copy-start(f32[1,1,512,256]{3,2,1,0:T(8,128)} %param.14) | copy-start | bytes 1572868
  194.9 5.3 %copy-start.10 = (f32[256,256]{1,0:T(8,128)S(1)}, f32[256,256]{1,0:T(8,128)}, u32[]{:S(2)}) copy-start(f32[256,256]{1,0:T(8,128)} %param.16) | copy-start | bytes 786436
  199.3 0.8 copy-start.5
  201.6 69.2 %all-gather.11.cloned.1.call-start = ((), (), s32[]{:S(2)}) async-start(), calls=%async_computation.9 | async-start | bytes 1572864 | tf_op jit(solution)/shard_map/while/body/eval_jaxpr/all_gather | solution.py:76
  227.5 3.5 copy-start.16
  227.5 3.5 copy-start.25
  227.5 3.5 copy-start.36
  231.0 15.4 %copy-start.6 = (f32[512,256]{1,0:T(8,128)S(1)}, f32[512,256]{1,0:T(8,128)}, u32[]{:S(2)}) copy-start(f32[512,256]{1,0:T(8,128)} %copy-done.5) | copy-start | bytes 1572868
  231.7 16.3 %copy-start.11 = (f32[256,256]{1,0:T(8,128)S(1)}, f32[256,256]{1,0:T(8,128)}, u32[]{:S(2)}) copy-start(f32[256,256]{1,0:T(8,128)} %param.16) | copy-start | bytes 786436
  231.7 14.7 %collective-permute-start.3 = (f32[512,256]{1,0:T(8,128)S(1)}, f32[512,256]{1,0:T(8,128)S(1)}, u32[]{:S(2)}, u32[]{:S(2)}) collective-permute-start(f32[512,256]{1,0:T(8,128)S(1)} %fusion.23), channel_id=1, source_target_pairs={{8,0},{16,8},{24,16},{9,1},{17,9},{25,17},{10,2},{18,10},{26,18},{... | collective-permute-start | bytes 1572872 | tf_op jit(solution)/shard_map/ppermute | solution.py:12
  246.4 0.8 copy-start.28
  247.2 0.8 copy-start.19
  249.4 69.2 %all-gather.13.cloned.1.call-start = ((), (), s32[]{:S(2)}) async-start(), calls=%async_computation.10 | async-start | bytes 1572864 | tf_op jit(solution)/shard_map/while/body/eval_jaxpr/all_gather | solution.py:76
  275.3 3.5 copy-start.17
  275.3 3.5 copy-start.26
  275.3 3.5 copy-start.29
  275.3 3.5 copy-start.33
  278.8 15.4 %copy-start.7 = (f32[512,256]{1,0:T(8,128)S(1)}, f32[512,256]{1,0:T(8,128)}, u32[]{:S(2)}) copy-start(f32[512,256]{1,0:T(8,128)} %copy-done.5) | copy-start | bytes 1572868
  279.6 16.3 %copy-start.12 = (f32[256,256]{1,0:T(8,128)S(1)}, f32[256,256]{1,0:T(8,128)}, u32[]{:S(2)}) copy-start(f32[256,256]{1,0:T(8,128)} %param.16) | copy-start | bytes 786436
  279.6 14.7 %collective-permute-start.4 = (f32[512,256]{1,0:T(8,128)S(1)}, f32[512,256]{1,0:T(8,128)S(1)}, u32[]{:S(2)}, u32[]{:S(2)}) collective-permute-start(f32[512,256]{1,0:T(8,128)S(1)} %add_add_fusion.1), channel_id=1, source_target_pairs={{8,0},{16,8},{24,16},{9,1},{17,9},{25,17},{10,2},{18,10},{26,18},{... | collective-permute-start | bytes 1572872 | tf_op jit(solution)/shard_map/ppermute | solution.py:12
  294.3 0.8 copy-start.30
  295.1 0.8 copy-start.20
  297.3 68.9 %all-gather.15.cloned.1.call-start = ((), (), s32[]{:S(2)}) async-start(), calls=%async_computation.11 | async-start | bytes 1572864 | tf_op jit(solution)/shard_map/while/body/eval_jaxpr/all_gather | solution.py:76
  323.2 3.5 copy-start.18
  323.2 3.5 copy-start.27
  323.2 3.5 copy-start.31
  323.2 3.5 copy-start.34
  326.7 15.5 %copy-start.4 = (f32[512,256]{1,0:T(8,128)S(1)}, f32[512,256]{1,0:T(8,128)}, u32[]{:S(2)}) copy-start(f32[512,256]{1,0:T(8,128)} %copy-done.3) | copy-start | bytes 1572868
  326.7 15.4 %copy-start.8 = (f32[512,256]{1,0:T(8,128)S(1)}, f32[512,256]{1,0:T(8,128)}, u32[]{:S(2)}) copy-start(f32[512,256]{1,0:T(8,128)} %copy-done.5) | copy-start | bytes 1572868
  327.5 15.9 %copy-start.13 = (f32[256,256]{1,0:T(8,128)S(1)}, f32[256,256]{1,0:T(8,128)}, u32[]{:S(2)}) copy-start(f32[256,256]{1,0:T(8,128)} %param.16) | copy-start | bytes 786436
  327.5 14.7 %collective-permute-start.5 = (f32[512,256]{1,0:T(8,128)S(1)}, f32[512,256]{1,0:T(8,128)S(1)}, u32[]{:S(2)}, u32[]{:S(2)}) collective-permute-start(f32[512,256]{1,0:T(8,128)S(1)} %add_add_fusion), channel_id=1, source_target_pairs={{8,0},{16,8},{24,16},{9,1},{17,9},{25,17},{10,2},{18,10},{26,18},{... | collective-permute-start | bytes 1572872 | tf_op jit(solution)/shard_map/ppermute | solution.py:12
  343.4 3.5 copy-start.32
  343.4 5.2 copy-start.35
  344.8 159.1 %all-reduce.3.cloned.1.call-start = ((), (), s32[]{:S(2)}) async-start(), calls=%async_computation.12 | async-start | bytes 2097152 | tf_op jit(solution)/shard_map/psum | solution.py:151
Sparse Core Ops, SparseCore 0:
  17.4 20.3 reduce-scatter.4
  70.5 21.2 reduce-scatter.6
  122.6 21.2 reduce-scatter.8
  173.6 21.2 reduce-scatter.10
  201.7 21.2 all-gather.8
  249.6 21.1 all-gather.10
  297.4 21.2 all-gather.12
  344.9 21.1 all-gather.14
  372.5 131.3 all-reduce.2
where the time goes:
time: 527 us; the launch traced here: 517 us
  waiting for transfers between devices  311 us (59%)
  matrix products  104 us (20%)
  blocking collectives  40.8 us (8%)
  local copies, waits for them, and re-layouts  23.6 us (4%)
  starting transfers between devices  18.3 us (3%)
  between operations  14.8 us (3%)
    psum x1, waiting for transfers between devices, on_device(): totals = lax.psum(weight_grads, ('tm', 'ent', 'batch'))  90.7 us
    reduce_scatter x4, waiting for transfers between devices, natural_step(): lax.psum_scatter(partial_value, 'ent', scatter_dimension=0, tiled=True)[0]  77.5 us
    all_gather x4, waiting for transfers between devices, natural_spread(): gathered = lax.all_gather(d_incoming[None], 'ent', axis=0, tiled=True)  71.8 us
    ppermute x6, waiting for transfers between devices, shifted(): lax.ppermute(value, axis, [(source, source + steps) for source in range(f...  71 us
    dot_general x26, matrix products, product(): return jnp.dot(left, right, precision=highest)  42.8 us
    psum x1, blocking collectives, on_device(): totals = lax.psum(weight_grads, ('tm', 'ent', 'batch'))  40.8 us
    dot_general x4, matrix products, natural_spread(): jnp.einsum('tg,gid->tid', dest_table(dst_t), gathered, precision=highest)  17.9 us
    ppermute x6, starting transfers between devices, shifted(): lax.ppermute(value, axis, [(source, source + steps) for source in range(f...  16.8 us
  transfers between devices with their start and end apart: 15, of which 15 were waited for; matrix products, arithmetic and copies ran while one was open for 4% of the time, Pallas kernels for 0%

commit v1 on v0

v1 whole, which is shorter than its diff:
```python
import functools

import jax
import jax.numpy as jnp
from jax import lax
from jax.experimental import pallas as pl
from jax.experimental.pallas import tpu as pltpu
from jax.sharding import PartitionSpec as P

MESH = pl.DeviceIdType.MESH
CHUNKS = 4
f32, bf16 = jnp.float32, jnp.bfloat16
NN = (((1,), (0,)), ((), ()))
NT = (((1,), (1,)), ((), ()))


def split(value):
    high = value.astype(bf16)
    return high, (value - high.astype(f32)).astype(bf16)


def dot3(left, right, dims=NN):
    one = functools.partial(
        lax.dot_general, dimension_numbers=dims, preferred_element_type=f32
    )
    return one(left[0], right[0]) + (one(left[0], right[1]) + one(left[1], right[0]))


def remote(src, dst, send, recv, axis, index):
    return pltpu.make_async_remote_copy(
        src_ref=src, dst_ref=dst, send_sem=send, recv_sem=recv,
        device_id={axis: index}, device_id_type=MESH,
    )


def step_kernel(
    n_tm, n_ent,
    dst_ref, rel_ref, init_ref, tiles_ref, cot_ref, emb_ref, wn_ref, ws_ref, wg_ref, bias_ref,
    states_ref, grel_ref, gneigh_ref, gself_ref, ggate_ref, gbias_ref,
    st, dz, dout, agg, upd, cand, proj, part, ysend, yrecv, dagg, grecv, msg_out, msg_in,
    th, tl, tth, ttl, wnh, wnl, wsh, wsl, wgh, wgl, sth, stl, agh, agl, coef_a, coef_b,
    dpre, dgate, dprev,
    ys_sem, yr_sem, gs_sem, gr_sem, ms_sem, mr_sem, zs_sem, zr_sem, bs_sem, br_sem,
):
    tm = lax.axis_index("tm")
    ent = lax.axis_index("ent")
    n_tile = tiles_ref.shape[0]
    rows, width = init_ref.shape
    step = rows // CHUNKS
    chunk = [slice(c * step, (c + 1) * step) for c in range(CHUNKS)]
    peers = [lax.rem(ent + off, n_ent) for off in range(n_ent)]
    up = jnp.minimum(tm + 1, n_tm - 1)
    down = jnp.maximum(tm - 1, 0)
    has_up, has_down = tm < n_tm - 1, tm > 0

    barrier = pltpu.get_barrier_semaphore()
    for off in range(1, n_ent):
        pl.semaphore_signal(barrier, inc=1, device_id={"ent": peers[off]}, device_id_type=MESH)

    @pl.when(has_up)
    def _():
        pl.semaphore_signal(barrier, inc=1, device_id={"tm": up}, device_id_type=MESH)

    @pl.when(has_down)
    def _():
        pl.semaphore_signal(barrier, inc=1, device_id={"tm": down}, device_id_type=MESH)

    for k in range(n_tile):
        th[k], tl[k] = split(tiles_ref[k])
    wnh[...], wnl[...] = split(wn_ref[...])
    wsh[...], wsl[...] = split(ws_ref[...])
    wgh[...], wgl[...] = split(wg_ref[...])
    wn, ws, wg = (wnh, wnl), (wsh, wsl), (wgh, wgl)

    def both(pair, *index):
        return tuple(ref[index] if index else ref[...] for ref in pair)

    @pl.when(tm == 0)
    def _():
        st[...] = init_ref[...]

    @pl.when(tm == n_tm - 1)
    def _():
        dz[...] = jnp.zeros_like(dz)

    pl.semaphore_wait(
        barrier, n_ent - 1 + has_up.astype(jnp.int32) + has_down.astype(jnp.int32)
    )

    hits = [
        [(dst_ref[k] == peers[off]).astype(f32) for k in range(n_tile)] for off in range(n_ent)
    ]
    rel_rows = [emb_ref[pl.ds(rel_ref[k], 1), :] for k in range(n_tile)]
    row_sums = [jnp.sum(tiles_ref[k], axis=1, keepdims=True) for k in range(n_tile)]
    for k in range(n_tile):
        part[k] = row_sums[k] * rel_rows[k]

    def y_copy(off, c):
        return remote(
            ysend.at[off - 1, chunk[c]], yrecv.at[off - 1, chunk[c]],
            ys_sem.at[off - 1, c], yr_sem.at[off - 1, c], "ent", peers[off],
        )

    def z_copy(c):
        return remote(
            states_ref.at[chunk[c]], st.at[chunk[c]], zs_sem.at[c], zr_sem.at[c], "tm", up
        )

    def project(c, pieces):
        proj[0, chunk[c]] = dot3(pieces, both(wg))
        proj[1, chunk[c]] = dot3(pieces, both(ws))

    for c in range(CHUNKS):

        @pl.when(has_down)
        def _():
            z_copy(c).wait_recv()

        pieces = split(st[chunk[c]])
        if c < CHUNKS - 1:
            for k in range(n_tile):
                part[k] += dot3(both((th, tl), k, slice(None), chunk[c]), pieces)
            project(c, pieces)
        else:
            for d in range(CHUNKS):
                done = [
                    part[k, chunk[d]] + dot3(both((th, tl), k, chunk[d], chunk[c]), pieces)
                    for k in range(n_tile)
                ]
                for off in range(1, n_ent):
                    ysend[off - 1, chunk[d]] = sum(
                        done[k] * hits[off][k] for k in range(n_tile)
                    )
                    y_copy(off, d).start()
                agg[chunk[d]] = sum(done[k] * hits[0][k] for k in range(n_tile))
            project(c, pieces)

    for c in range(CHUNKS):
        total = agg[chunk[c]]
        for off in range(1, n_ent):
            y_copy(off, c).wait_recv()
            total = total + yrecv[off - 1, chunk[c]]
        agg[chunk[c]] = total
        u = jax.nn.sigmoid(proj[0, chunk[c]] + bias_ref[...])
        v = jnp.tanh(dot3(split(total), both(wn)) + proj[1, chunk[c]])
        states_ref[chunk[c]] = u * v + (1.0 - u) * st[chunk[c]]

        @pl.when(has_up)
        def _():
            z_copy(c).start()

        upd[chunk[c]] = u
        cand[chunk[c]] = v

    for k in range(n_tile):
        turned = tiles_ref[k].T
        sums = jnp.sum(turned, axis=0, keepdims=True)
        tth[k], ttl[k] = split(turned)
        for off in range(n_ent):
            target = msg_in if off == 0 else msg_out
            target[off, k : k + 1] = sums * hits[off][k]
            target[off, n_tile + k : n_tile + k + 1] = jnp.full_like(
                sums, rel_ref[k].astype(f32)
            )
    for off in range(n_ent):
        target = msg_in if off == 0 else msg_out
        if target.shape[1] > 2 * n_tile:
            target[off, 2 * n_tile :] = jnp.zeros(
                (target.shape[1] - 2 * n_tile, target.shape[2]), f32
            )

    def m_copy(off):
        return remote(
            msg_out.at[off], msg_in.at[off], ms_sem.at[off - 1], mr_sem.at[off - 1],
            "ent", peers[off],
        )

    for off in range(1, n_ent):
        m_copy(off).start()
    sth[...], stl[...] = split(st[...].T)
    agh[...], agl[...] = split(agg[...].T)
    u, v = upd[...], cand[...]
    coef_a[...] = u * (1.0 - v * v)
    coef_b[...] = (v - st[...]) * u * (1.0 - u)

    def g_copy(off, c):
        return remote(
            dagg.at[chunk[c]], grecv.at[off - 1, chunk[c]],
            gs_sem.at[off - 1, c], gr_sem.at[off - 1, c], "ent", peers[off],
        )

    def b_copy(c):
        return remote(dout.at[chunk[c]], dz.at[chunk[c]], bs_sem.at[c], br_sem.at[c], "tm", down)

    for c in range(CHUNKS):

        @pl.when(has_up)
        def _():
            b_copy(c).wait_recv()

        dnew = dz[chunk[c]] + cot_ref[chunk[c]]
        pre = dnew * coef_a[chunk[c]]
        gate = dnew * coef_b[chunk[c]]
        pre_pieces = split(pre)
        dagg[chunk[c]] = dot3(pre_pieces, both(wn), NT)

        @pl.when(has_down)
        def _():
            for off in range(1, n_ent):
                g_copy(off, c).start()

        dpre[chunk[c]] = pre
        dgate[chunk[c]] = gate

        @pl.when(has_down)
        def _():
            dprev[chunk[c]] = (
                dnew * (1.0 - upd[chunk[c]])
                + dot3(pre_pieces, both(ws), NT)
                + dot3(split(gate), both(wg), NT)
            )

    @pl.when(has_down)
    def _():
        for c in range(CHUNKS):
            own = dagg[chunk[c]]
            spread = [own * hits[0][k] for k in range(n_tile)]
            for off in range(1, n_ent):
                g_copy(off, c).wait_recv()
                other = grecv[off - 1, chunk[c]]
                for k in range(n_tile):
                    spread[k] = spread[k] + other * hits[n_ent - off][k]
            pieces = [split(spread[k]) for k in range(n_tile)]
            if c < CHUNKS - 1:
                dprev[...] += sum(
                    dot3(both((tth, ttl), k, slice(None), chunk[c]), pieces[k])
                    for k in range(n_tile)
                )
            else:
                for d in range(CHUNKS):
                    dout[chunk[d]] = dprev[chunk[d]] + sum(
                        dot3(both((tth, ttl), k, chunk[d], chunk[c]), pieces[k])
                        for k in range(n_tile)
                    )
                    b_copy(d).start()

    pre_pieces, gate_pieces = split(dpre[...]), split(dgate[...])
    gneigh_ref[...] = dot3(both((agh, agl)), pre_pieces)
    gself_ref[...] = dot3(both((sth, stl)), pre_pieces)
    ggate_ref[...] = dot3(both((sth, stl)), gate_pieces)
    gbias_ref[...] = jnp.sum(dgate[...], axis=0, keepdims=True)
    grad_pieces = split(dagg[...])
    number = lax.broadcasted_iota(jnp.int32, grel_ref.shape, 0).astype(f32)
    grad_rel = jnp.zeros(grel_ref.shape, f32)
    for off in range(n_ent):
        if off > 0:
            m_copy(off).wait_recv()
        found = dot3(split(msg_in[off]), grad_pieces)
        for k in range(n_tile):
            place = msg_in[off, n_tile + k : n_tile + k + 1, 0:1]
            grad_rel = grad_rel + jnp.where(number == place, found[k : k + 1], 0.0)
    grel_ref[...] = grad_rel

    for off in range(1, n_ent):
        m_copy(off).wait_send()
        for c in range(CHUNKS):
            y_copy(off, c).wait_send()

    @pl.when(has_up)
    def _():
        for c in range(CHUNKS):
            z_copy(c).wait_send()

    @pl.when(has_down)
    def _():
        for c in range(CHUNKS):
            b_copy(c).wait_send()
            for off in range(1, n_ent):
                g_copy(off, c).wait_send()


def on_device(
    n_tm, n_ent,
    init_state, tiles, dst_block, rel_id, cotangent, rel_emb, w_neigh, w_self, w_gate, b_gate
):
    assert tiles.shape[:2] == (1, 1)
    n_tile, rows = tiles.shape[2], tiles.shape[3]
    width, n_rel = init_state.shape[2], rel_emb.shape[0]
    lines = -(-2 * n_tile // 8) * 8
    others = max(n_ent - 1, 1)
    square, flat = (n_tile, rows, rows), (rows, width)
    vmem = pltpu.VMEM
    sems = pltpu.SemaphoreType.DMA
    whole, small = pl.BlockSpec(memory_space=pltpu.VMEM), pl.BlockSpec(memory_space=pltpu.SMEM)
    shape = lambda *dims: jax.ShapeDtypeStruct(dims, f32)
    weight = (width, width)
    outs = pl.pallas_call(
        functools.partial(step_kernel, n_tm, n_ent),
        out_shape=(
            shape(rows, width), shape(n_rel, width), shape(*weight), shape(*weight),
            shape(*weight), shape(1, width),
        ),
        in_specs=[small, small] + [whole] * 8,
        out_specs=(whole,) * 6,
        scratch_shapes=[
            vmem(flat, f32), vmem(flat, f32), vmem(flat, f32), vmem(flat, f32),
            vmem(flat, f32), vmem(flat, f32), vmem((2,) + flat, f32),
            vmem((n_tile,) + flat, f32),
            vmem((others,) + flat, f32), vmem((others,) + flat, f32),
            vmem(flat, f32), vmem((others,) + flat, f32),
            vmem((n_ent, lines, rows), f32), vmem((n_ent, lines, rows), f32),
            vmem(square, bf16), vmem(square, bf16), vmem(square, bf16), vmem(square, bf16),
            vmem(weight, bf16), vmem(weight, bf16), vmem(weight, bf16), vmem(weight, bf16),
            vmem(weight, bf16), vmem(weight, bf16),
            vmem((width, rows), bf16), vmem((width, rows), bf16),
            vmem((width, rows), bf16), vmem((width, rows), bf16),
            vmem(flat, f32), vmem(flat, f32), vmem(flat, f32), vmem(flat, f32), vmem(flat, f32),
            sems((others, CHUNKS)), sems((others, CHUNKS)),
            sems((others, CHUNKS)), sems((others, CHUNKS)),
            sems((others,)), sems((others,)),
            sems((CHUNKS,)), sems((CHUNKS,)), sems((CHUNKS,)), sems((CHUNKS,)),
        ],
        compiler_params=pltpu.CompilerParams(
            collective_id=0, has_side_effects=True, vmem_limit_bytes=60 * 1024 * 1024
        ),
    )(
        dst_block[0, 0], rel_id[0, 0], init_state[0], tiles[0, 0], cotangent[0, 0],
        rel_emb, w_neigh, w_self, w_gate, b_gate[None],
    )
    totals = lax.psum(outs[1:], ("tm", "ent", "batch"))
    return (outs[0][None, None], totals[0], totals[1], totals[2], totals[3], totals[4][0])


def solution(mesh):
    placed = (
        P("batch", "ent", None),
        P("batch", "tm", "ent", None, None),
        P("batch", "tm", "ent"),
        P("batch", "tm", "ent"),
        P("batch", "tm", "ent", None),
        P(),
        P(),
        P(),
        P(),
        P(),
    )
    return jax.shard_map(
        functools.partial(on_device, mesh.shape["tm"], mesh.shape["ent"]),
        mesh=mesh,
        in_specs=placed,
        out_specs=(P("batch", "tm", "ent", None), P(), P(), P(), P(), P()),
        check_vma=False,
    )
```

time: 527 us -> 271 us (0.51); the launches traced: 517 us -> 268 us
  waiting for transfers between devices: 311 us -> 89.2 us
  Pallas kernels: 0 us -> 109 us
  matrix products: 104 us -> 0 us
  starting transfers between devices: 18.3 us -> 0.04 us
  local copies, waits for them, and re-layouts: 23.6 us -> 6.67 us
  blocking collectives: 40.8 us -> 48.6 us
    pallas_call x0 -> x1, Pallas kernels: none -> 109 us  [on_device(): pl.pallas_call(functools.partial(step_kernel, n_tm, n_ent), out_shape=(sh...]
    dot_general x43 -> x0, matrix products: 104 us -> none  [the longest x26 42.8 us: product(): return jnp.dot(left, right, precision=highest)]
    reduce_scatter x4 -> x0, waiting for transfers between devices: 77.5 us -> none  [natural_step(): lax.psum_scatter(partial_value, 'ent', scatter_dimension=0, tiled=True)[0]]
    all_gather x4 -> x0, waiting for transfers between devices: 71.8 us -> none  [natural_spread(): gathered = lax.all_gather(d_incoming[None], 'ent', axis=0, tiled=True)]
    ppermute x6 -> x0, waiting for transfers between devices: 71 us -> none  [shifted(): lax.ppermute(value, axis, [(source, source + steps) for source in range(f...]
    ppermute x6 -> x0, starting transfers between devices: 16.8 us -> none  [shifted(): lax.ppermute(value, axis, [(source, source + steps) for source in range(f...]
    dot_general x7 -> x0, local copies, waits for them, and re-layouts: 11.1 us -> none  [the longest x3 6.75 us: block_terms(): result = jnp.einsum('tij,jd->tid', tiles_t, current, precision=highest)]
    psum x1, blocking collectives: 40.8 us -> 48.6 us  [on_device(): totals = lax.psum(outs[1:], ('tm', 'ent', 'batch'))]
  transfers between devices with their start and end apart: 15 -> 1, of which waited for: 15 -> 1; matrix products, arithmetic and copies ran while one was open for 4% -> 0% of each run, Pallas kernels for 0% -> 0%
where the time goes in v1:
time: 271 us; the launch traced here: 268 us
  Pallas kernels  109 us (40%)
  waiting for transfers between devices  89.2 us (33%)
  blocking collectives  48.6 us (18%)
  between operations  14 us (5%)
  local copies, waits for them, and re-layouts  6.67 us (2%)
    pallas_call x1, Pallas kernels, on_device(): pl.pallas_call(functools.partial(step_kernel, n_tm, n_ent), out_shape=(sh...  109 us
    psum x1, waiting for transfers between devices, on_device(): totals = lax.psum(outs[1:], ('tm', 'ent', 'batch'))  89.2 us
    psum x1, blocking collectives, on_device(): totals = lax.psum(outs[1:], ('tm', 'ent', 'batch'))  48.6 us
    unnamed x9, local copies, waits for them, and re-layouts  6.67 us
  transfers between devices with their start and end apart: 1, of which 1 were waited for; matrix products, arithmetic and copies ran while one was open for 0% of the time, Pallas kernels for 0%

profile of v1, /device:TPU:13, one launch (start us, length us, event | category | flops | bytes accessed | tf_op | source)
XLA Modules:
  0.0 267.9 jit_solution(10898656721659103632)
XLA Ops:
  7.2 0.0 all-reduce.3.cloned.1.call-start
  7.2 109.3 %shard_map.145 = (f32[512,256]{1,0:T(8,128)}, f32[256,256]{1,0:T(8,128)}, f32[256,256]{1,0:T(8,128)}, f32[256,256]{1,0:T(8,128)}, f32[256,256]{1,0:T(8,128)}, /*index=5*/f32[1,256]{1,0:T(1,128)}) custom-call(s32[2]{0:T(128)} %bitcast.14, s32[2]{0:T(128)} %bitcast.15, f32[512,256]{1,0:T(8,128)} %bitcast.10, f32[2,512,512]{2,1,0:T(8,128)} %bitcast.8, ...), custom_call_target="tpu_custom_call" | custom-call | tf_op jit(solution)/shard_map/pallas_call | solution.py:297
  116.6 0.0 all-reduce.3.cloned.1.call-update
  116.6 48.6 %psum.39 = f32[256]{0:T(256)} all-reduce(f32[256]{0:T(256)} %bitcast.12), channel_id=1, replica_groups=mesh['tm'=4,'ent'=2,'batch'=4] {'tm','ent','batch'}, use_global_device_ids=true, to_apply=%region_4.0 | all-reduce | flops 256 | bytes 2048 | tf_op jit(solution)/shard_map/psum | solution.py:330
  165.2 89.2 %all-reduce.3.cloned.1.call-done = (f32[256,256]{1,0:T(8,128)}, f32[256,256]{1,0:T(8,128)}, f32[256,256]{1,0:T(8,128)}, f32[256,256]{1,0:T(8,128)}) async-done(((f32[256,256]{1,0:T(8,128)}, f32[256,256]{1,0:T(8,128)}, f32[256,256]{1,0:T(8,128)}, f32[256,256]{1,0:T(8,128)}), (f32[256,256]{1,0:T(8,128)}, f32[256,256]{1,0:T(8,128)}, f32[256,256]{1,0:T(8,128)}, ...) | async-done | bytes 1048592 | tf_op jit(solution)/shard_map/psum | solution.py:330
  254.4 0.0 copy-start.1
  254.4 0.0 copy-start
  254.4 1.9 copy.25
  256.3 1.7 copy.26
  258.0 1.7 copy.27
  259.6 0.0 copy-done.1
  259.6 0.7 copy.28
  260.3 0.0 copy-done
  260.3 0.7 copy.29
Async XLA Ops:
  7.2 247.2 %all-reduce.3.cloned.1.call-start = ((), (), s32[]{:S(2)}) async-start(), calls=%async_computation | async-start | bytes 2097152 | tf_op jit(solution)/shard_map/psum | solution.py:330
  254.4 5.3 %copy-start.1 = (f32[256,256]{1,0:T(8,128)S(1)}, f32[256,256]{1,0:T(8,128)}, u32[]{:S(2)}) copy-start(f32[256,256]{1,0:T(8,128)} %get-tuple-element.31) | copy-start | bytes 786436
  254.4 6.0 %copy-start = (f32[256,256]{1,0:T(8,128)S(1)}, f32[256,256]{1,0:T(8,128)}, u32[]{:S(2)}) copy-start(f32[256,256]{1,0:T(8,128)} %get-tuple-element.32) | copy-start | bytes 786436
Sparse Core Ops, SparseCore 0:
  116.7 137.6 all-reduce.2

commit v2 on v1

--- a/solution.py
+++ b/solution.py
@@ -34,13 +34,15 @@
 
 
 def step_kernel(
-    n_tm, n_ent,
+    n_tm, n_ent, n_batch,
     dst_ref, rel_ref, init_ref, tiles_ref, cot_ref, emb_ref, wn_ref, ws_ref, wg_ref, bias_ref,
     states_ref, grel_ref, gneigh_ref, gself_ref, ggate_ref, gbias_ref,
     st, dz, dout, agg, upd, cand, proj, part, ysend, yrecv, dagg, grecv, msg_out, msg_in,
     th, tl, tth, ttl, wnh, wnl, wsh, wsl, wgh, wgl, sth, stl, agh, agl, coef_a, coef_b,
     dpre, dgate, dprev,
+    grads, pair_in, half_sum, plane_in, chain_in, chain_out, final,
     ys_sem, yr_sem, gs_sem, gr_sem, ms_sem, mr_sem, zs_sem, zr_sem, bs_sem, br_sem,
+    one_sem, rs_sem, rr_sem, cs_sem, as_sem, ar_sem,
 ):
     tm = lax.axis_index("tm")
     ent = lax.axis_index("ent")
@@ -53,17 +55,25 @@
     down = jnp.maximum(tm - 1, 0)
     has_up, has_down = tm < n_tm - 1, tm > 0
 
+    batch = lax.axis_index("batch")
+    side = lax.rem(batch, 2)
+    pair = {"batch": batch + 1 - 2 * side}
+    members = n_batch // 2 * n_ent
+    member = batch // 2 * n_ent + ent
+    size = plane_in.shape[1]
+
+    def mate(distance):
+        index = lax.rem(member + distance + members, members)
+        return index, {"batch": index // n_ent * 2 + side, "ent": lax.rem(index, n_ent)}
+
     barrier = pltpu.get_barrier_semaphore()
-    for off in range(1, n_ent):
-        pl.semaphore_signal(barrier, inc=1, device_id={"ent": peers[off]}, device_id_type=MESH)
-
-    @pl.when(has_up)
-    def _():
-        pl.semaphore_signal(barrier, inc=1, device_id={"tm": up}, device_id_type=MESH)
-
-    @pl.when(has_down)
-    def _():
-        pl.semaphore_signal(barrier, inc=1, device_id={"tm": down}, device_id_type=MESH)
+    for q in range(1, members):
+        pl.semaphore_signal(barrier, inc=1, device_id=mate(q)[1], device_id_type=MESH)
+    pl.semaphore_signal(barrier, inc=1, device_id=pair, device_id_type=MESH)
+    for q in range(1, n_tm):
+        pl.semaphore_signal(
+            barrier, inc=1, device_id={"tm": lax.rem(tm + q, n_tm)}, device_id_type=MESH
+        )
 
     for k in range(n_tile):
         th[k], tl[k] = split(tiles_ref[k])
@@ -83,9 +93,7 @@
     def _():
         dz[...] = jnp.zeros_like(dz)
 
-    pl.semaphore_wait(
-        barrier, n_ent - 1 + has_up.astype(jnp.int32) + has_down.astype(jnp.int32)
-    )
+    pl.semaphore_wait(barrier, members + n_tm - 1)
 
     hits = [
         [(dst_ref[k] == peers[off]).astype(f32) for k in range(n_tile)] for off in range(n_ent)
@@ -245,10 +253,13 @@
                     b_copy(d).start()
 
     pre_pieces, gate_pieces = split(dpre[...]), split(dgate[...])
-    gneigh_ref[...] = dot3(both((agh, agl)), pre_pieces)
-    gself_ref[...] = dot3(both((sth, stl)), pre_pieces)
-    ggate_ref[...] = dot3(both((sth, stl)), gate_pieces)
-    gbias_ref[...] = jnp.sum(dgate[...], axis=0, keepdims=True)
+    n_rel = grel_ref.shape[0]
+    base = [n_rel + width * i for i in range(4)]
+    grads[base[0] : base[1]] = dot3(both((agh, agl)), pre_pieces)
+    grads[base[1] : base[2]] = dot3(both((sth, stl)), pre_pieces)
+    grads[base[2] : base[3]] = dot3(both((sth, stl)), gate_pieces)
+    grads[base[3] :] = jnp.zeros((grads.shape[0] - base[3], width), f32)
+    grads[base[3] : base[3] + 1] = jnp.sum(dgate[...], axis=0, keepdims=True)
     grad_pieces = split(dagg[...])
     number = lax.broadcasted_iota(jnp.int32, grel_ref.shape, 0).astype(f32)
     grad_rel = jnp.zeros(grel_ref.shape, f32)
@@ -259,7 +270,105 @@
         for k in range(n_tile):
             place = msg_in[off, n_tile + k : n_tile + k + 1, 0:1]
             grad_rel = grad_rel + jnp.where(number == place, found[k : k + 1], 0.0)
-    grel_ref[...] = grad_rel
+    grads[:n_rel] = grad_rel
+
+    def move(src, dst, send, recv, target):
+        return pltpu.make_async_remote_copy(
+            src_ref=src, dst_ref=dst, send_sem=send, recv_sem=recv,
+            device_id=target, device_id_type=MESH,
+        )
+
+    half = members * size
+    cross = move(
+        grads.at[pl.ds(pl.multiple_of((1 - side) * half, 8), half)], pair_in,
+        one_sem.at[0], one_sem.at[1], pair,
+    )
+    cross.start()
+    cross.wait_recv()
+    half_sum[...] = grads[pl.ds(pl.multiple_of(side * half, 8), half)] + pair_in[...]
+
+    def shard(index):
+        return pl.ds(pl.multiple_of(index * size, 8), size)
+
+    def scatter(q):
+        index, target = mate(q)
+        return move(
+            half_sum.at[shard(index)], plane_in.at[q - 1], rs_sem.at[q - 1], rr_sem.at[q - 1],
+            target,
+        )
+
+    for q in range(1, members):
+        scatter(q).start()
+    total = half_sum[shard(member)]
+    for q in range(1, members):
+        scatter(q).wait_recv()
+        total = total + plane_in[q - 1]
+    chain_out[...] = total
+    chain = move(chain_out, chain_in, one_sem.at[2], one_sem.at[3], {"tm": down})
+
+    @pl.when(has_up)
+    def _():
+        chain.wait_recv()
+        chain_out[...] += chain_in[...]
+
+    @pl.when(has_down)
+    def _():
+        chain.start()
+
+    place = shard(side * members + member)
+
+    def spread_copy(t):
+        return move(
+            final.at[place], final.at[place], cs_sem.at[t - 1], one_sem.at[4], {"tm": t}
+        )
+
+    @pl.when(tm == 0)
+    def _():
+        final[place] = chain_out[...]
+        for t in range(n_tm - 1, 0, -1):
+            spread_copy(t).start()
+
+    @pl.when(has_down)
+    def _():
+        spread_copy(1).wait_recv()
+
+    def gather(q, index):
+        where = shard(side * members + index)
+        return move(
+            final.at[where], final.at[where], as_sem.at[q - 1], ar_sem.at[q - 1], mate(q)[1]
+        )
+
+    for q in range(1, members):
+        gather(q, member).start()
+    for q in range(1, members):
+        gather(q, mate(-q)[0]).wait_recv()
+
+    def swap(which):
+        where = pl.ds(pl.multiple_of(which * half, 8), half)
+        return move(final.at[where], final.at[where], one_sem.at[5], one_sem.at[6], pair)
+
+    swap(side).start()
+    swap(1 - side).wait_recv()
+    grel_ref[...] = final[:n_rel]
+    gneigh_ref[...] = final[base[0] : base[1]]
+    gself_ref[...] = final[base[1] : base[2]]
+    ggate_ref[...] = final[base[2] : base[3]]
+    gbias_ref[...] = final[base[3] : base[3] + 1]
+
+    cross.wait_send()
+    swap(side).wait_send()
+    for q in range(1, members):
+        scatter(q).wait_send()
+        gather(q, member).wait_send()
+
+    @pl.when(has_down)
+    def _():
+        chain.wait_send()
+
+    @pl.when(tm == 0)
+    def _():
+        for t in range(1, n_tm):
+            spread_copy(t).wait_send()
 
     for off in range(1, n_ent):
         m_copy(off).wait_send()
@@ -280,7 +389,7 @@
 
 
 def on_device(
-    n_tm, n_ent,
+    n_tm, n_ent, n_batch,
     init_state, tiles, dst_block, rel_id, cotangent, rel_emb, w_neigh, w_self, w_gate, b_gate
 ):
     assert tiles.shape[:2] == (1, 1)
@@ -288,6 +397,10 @@
     width, n_rel = init_state.shape[2], rel_emb.shape[0]
     lines = -(-2 * n_tile // 8) * 8
     others = max(n_ent - 1, 1)
+    members = n_batch // 2 * n_ent
+    shards = 2 * members
+    size = -(-(n_rel + 3 * width + 8) // (8 * shards)) * 8
+    mates = max(members - 1, 1)
     square, flat = (n_tile, rows, rows), (rows, width)
     vmem = pltpu.VMEM
     sems = pltpu.SemaphoreType.DMA
@@ -295,7 +408,7 @@
     shape = lambda *dims: jax.ShapeDtypeStruct(dims, f32)
     weight = (width, width)
     outs = pl.pallas_call(
-        functools.partial(step_kernel, n_tm, n_ent),
+        functools.partial(step_kernel, n_tm, n_ent, n_batch),
         out_shape=(
             shape(rows, width), shape(n_rel, width), shape(*weight), shape(*weight),
             shape(*weight), shape(1, width),
@@ -315,10 +428,16 @@
             vmem((width, rows), bf16), vmem((width, rows), bf16),
             vmem((width, rows), bf16), vmem((width, rows), bf16),
             vmem(flat, f32), vmem(flat, f32), vmem(flat, f32), vmem(flat, f32), vmem(flat, f32),
+            vmem((shards * size, width), f32), vmem((members * size, width), f32),
+            vmem((members * size, width), f32), vmem((mates, size, width), f32),
+            vmem((size, width), f32), vmem((size, width), f32),
+            vmem((shards * size, width), f32),
             sems((others, CHUNKS)), sems((others, CHUNKS)),
             sems((others, CHUNKS)), sems((others, CHUNKS)),
             sems((others,)), sems((others,)),
             sems((CHUNKS,)), sems((CHUNKS,)), sems((CHUNKS,)), sems((CHUNKS,)),
+            sems((7,)), sems((mates,)), sems((mates,)), sems((n_tm,)),
+            sems((mates,)), sems((mates,)),
         ],
         compiler_params=pltpu.CompilerParams(
             collective_id=0, has_side_effects=True, vmem_limit_bytes=60 * 1024 * 1024
@@ -327,8 +446,7 @@
         dst_block[0, 0], rel_id[0, 0], init_state[0], tiles[0, 0], cotangent[0, 0],
         rel_emb, w_neigh, w_self, w_gate, b_gate[None],
     )
-    totals = lax.psum(outs[1:], ("tm", "ent", "batch"))
-    return (outs[0][None, None], totals[0], totals[1], totals[2], totals[3], totals[4][0])
+    return (outs[0][None, None],) + tuple(outs[1:5]) + (outs[5][0],)
 
 
 def solution(mesh):
@@ -345,7 +463,7 @@
         P(),
     )
     return jax.shard_map(
-        functools.partial(on_device, mesh.shape["tm"], mesh.shape["ent"]),
+        functools.partial(on_device, *(mesh.shape[name] for name in ("tm", "ent", "batch"))),
         mesh=mesh,
         in_specs=placed,
         out_specs=(P("batch", "tm", "ent", None), P(), P(), P(), P(), P()),

time: 271 us -> 158 us (0.58); the launches traced: 268 us -> 158 us
  waiting for transfers between devices: 89.2 us -> 0 us
  blocking collectives: 48.6 us -> 0 us
  Pallas kernels: 109 us -> 150 us
  between operations: 14 us -> 0.67 us
    psum x1 -> x0, waiting for transfers between devices: 89.2 us -> none  [on_device(): totals = lax.psum(outs[1:], ('tm', 'ent', 'batch'))]
    psum x1 -> x0, blocking collectives: 48.6 us -> none  [on_device(): totals = lax.psum(outs[1:], ('tm', 'ent', 'batch'))]
    pallas_call x1, Pallas kernels: 109 us -> 150 us  [on_device(): pl.pallas_call(functools.partial(step_kernel, n_tm, n_ent, n_batch), out_...]
    unnamed x9 -> x12, local copies, waits for them, and re-layouts: 6.67 us -> 7.24 us
  transfers between devices with their start and end apart: 1 -> 0, of which waited for: 1 -> 0; matrix products, arithmetic and copies ran while one was open for 0% -> 0% of each run, Pallas kernels for 0% -> 0%
where the time goes in v2:
time: 158 us
  Pallas kernels  150 us (95%)
  local copies, waits for them, and re-layouts  7.24 us (5%)
    pallas_call x1, Pallas kernels, on_device(): pl.pallas_call(functools.partial(step_kernel, n_tm, n_ent, n_batch), out_...  150 us
    unnamed x12, local copies, waits for them, and re-layouts  7.24 us

profile of v2, /device:TPU:13, one launch (start us, length us, event | category | flops | bytes accessed | tf_op | source)
XLA Modules:
  0.0 158.3 jit_solution(1775624098197383232)
XLA Ops:
  0.6 150.3 %shard_map.145 = (f32[512,256]{1,0:T(8,128)}, f32[256,256]{1,0:T(8,128)}, f32[256,256]{1,0:T(8,128)}, f32[256,256]{1,0:T(8,128)}, f32[256,256]{1,0:T(8,128)}, /*index=5*/f32[1,256]{1,0:T(1,128)}) custom-call(s32[2]{0:T(128)} %bitcast.14, s32[2]{0:T(128)} %bitcast.15, f32[512,256]{1,0:T(8,128)} %bitcast.10, f32[2,512,512]{2,1,0:T(8,128)} %bitcast.8, ...), custom_call_target="tpu_custom_call" | custom-call | tf_op jit(solution)/shard_map/pallas_call | solution.py:410
  151.0 0.0 copy-start.1
  151.0 0.0 copy-start
  151.0 0.0 copy-start.2
  151.0 1.9 %copy.22 = f32[1,1,512,256]{3,2,1,0:T(8,128)} copy(f32[1,1,512,256]{3,2,1,0:T(8,128)} %bitcast.9) | data formatting | bytes 1048576
  152.9 1.7 %copy.23 = f32[256,256]{1,0:T(8,128)} copy(f32[256,256]{1,0:T(8,128)} %get-tuple-element.25) | data formatting | bytes 524288
  154.6 1.7 %copy.24 = f32[256,256]{1,0:T(8,128)} copy(f32[256,256]{1,0:T(8,128)} %get-tuple-element.26) | data formatting | bytes 524288
  156.3 0.0 copy-done.1
  156.3 0.7 copy.25
  157.0 0.0 copy-done
  157.0 0.7 copy.26
  157.7 0.0 copy-done.2
  157.7 0.6 copy.27
Async XLA Ops:
  151.0 5.3 %copy-start.1 = (f32[256,256]{1,0:T(8,128)S(1)}, f32[256,256]{1,0:T(8,128)}, u32[]{:S(2)}) copy-start(f32[256,256]{1,0:T(8,128)} %get-tuple-element.27) | copy-start | bytes 786436
  151.0 6.0 %copy-start = (f32[256,256]{1,0:T(8,128)S(1)}, f32[256,256]{1,0:T(8,128)}, u32[]{:S(2)}) copy-start(f32[256,256]{1,0:T(8,128)} %get-tuple-element.28) | copy-start | bytes 786436
  151.0 6.7 %copy-start.2 = (f32[1,256]{1,0:T(1,128)S(1)}, f32[1,256]{1,0:T(1,128)}, u32[]{:S(2)}) copy-start(f32[1,256]{1,0:T(1,128)} %get-tuple-element.17) | copy-start | bytes 3076

commit v3 on v2

--- a/solution.py
+++ b/solution.py
@@ -9,6 +9,7 @@
 
 MESH = pl.DeviceIdType.MESH
 CHUNKS = 4
+PIECES = 8
 f32, bf16 = jnp.float32, jnp.bfloat16
 NN = (((1,), (0,)), ((), ()))
 NT = (((1,), (1,)), ((), ()))
@@ -50,6 +51,9 @@
     rows, width = init_ref.shape
     step = rows // CHUNKS
     chunk = [slice(c * step, (c + 1) * step) for c in range(CHUNKS)]
+    fine = rows // PIECES
+    piece = [slice(p * fine, (p + 1) * fine) for p in range(PIECES)]
+    inside = [range(c * PIECES // CHUNKS, (c + 1) * PIECES // CHUNKS) for c in range(CHUNKS)]
     peers = [lax.rem(ent + off, n_ent) for off in range(n_ent)]
     up = jnp.minimum(tm + 1, n_tm - 1)
     down = jnp.maximum(tm - 1, 0)
@@ -105,13 +109,13 @@
 
     def y_copy(off, c):
         return remote(
-            ysend.at[off - 1, chunk[c]], yrecv.at[off - 1, chunk[c]],
+            ysend.at[off - 1, piece[c]], yrecv.at[off - 1, piece[c]],
             ys_sem.at[off - 1, c], yr_sem.at[off - 1, c], "ent", peers[off],
         )
 
     def z_copy(c):
         return remote(
-            states_ref.at[chunk[c]], st.at[chunk[c]], zs_sem.at[c], zr_sem.at[c], "tm", up
+            states_ref.at[piece[c]], st.at[piece[c]], zs_sem.at[c], zr_sem.at[c], "tm", up
         )
 
     def project(c, pieces):
@@ -122,7 +126,8 @@
 
         @pl.when(has_down)
         def _():
-            z_copy(c).wait_recv()
+            for p in inside[c]:
+                z_copy(p).wait_recv()
 
         pieces = split(st[chunk[c]])
         if c < CHUNKS - 1:
@@ -130,35 +135,35 @@
                 part[k] += dot3(both((th, tl), k, slice(None), chunk[c]), pieces)
             project(c, pieces)
         else:
-            for d in range(CHUNKS):
+            for d in range(PIECES):
                 done = [
-                    part[k, chunk[d]] + dot3(both((th, tl), k, chunk[d], chunk[c]), pieces)
+                    part[k, piece[d]] + dot3(both((th, tl), k, piece[d], chunk[c]), pieces)
                     for k in range(n_tile)
                 ]
                 for off in range(1, n_ent):
-                    ysend[off - 1, chunk[d]] = sum(
+                    ysend[off - 1, piece[d]] = sum(
                         done[k] * hits[off][k] for k in range(n_tile)
                     )
                     y_copy(off, d).start()
-                agg[chunk[d]] = sum(done[k] * hits[0][k] for k in range(n_tile))
+                agg[piece[d]] = sum(done[k] * hits[0][k] for k in range(n_tile))
             project(c, pieces)
 
-    for c in range(CHUNKS):
-        total = agg[chunk[c]]
+    for c in range(PIECES):
+        total = agg[piece[c]]
         for off in range(1, n_ent):
             y_copy(off, c).wait_recv()
-            total = total + yrecv[off - 1, chunk[c]]
-        agg[chunk[c]] = total
-        u = jax.nn.sigmoid(proj[0, chunk[c]] + bias_ref[...])
-        v = jnp.tanh(dot3(split(total), both(wn)) + proj[1, chunk[c]])
-        states_ref[chunk[c]] = u * v + (1.0 - u) * st[chunk[c]]
+            total = total + yrecv[off - 1, piece[c]]
+        agg[piece[c]] = total
+        u = jax.nn.sigmoid(proj[0, piece[c]] + bias_ref[...])
+        v = jnp.tanh(dot3(split(total), both(wn)) + proj[1, piece[c]])
+        states_ref[piece[c]] = u * v + (1.0 - u) * st[piece[c]]
 
         @pl.when(has_up)
         def _():
             z_copy(c).start()
 
-        upd[chunk[c]] = u
-        cand[chunk[c]] = v
+        upd[piece[c]] = u
+        cand[piece[c]] = v
 
     for k in range(n_tile):
         turned = tiles_ref[k].T
@@ -193,37 +198,37 @@
 
     def g_copy(off, c):
         return remote(
-            dagg.at[chunk[c]], grecv.at[off - 1, chunk[c]],
+            dagg.at[piece[c]], grecv.at[off - 1, piece[c]],
             gs_sem.at[off - 1, c], gr_sem.at[off - 1, c], "ent", peers[off],
         )
 
     def b_copy(c):
-        return remote(dout.at[chunk[c]], dz.at[chunk[c]], bs_sem.at[c], br_sem.at[c], "tm", down)
-
-    for c in range(CHUNKS):
+        return remote(dout.at[piece[c]], dz.at[piece[c]], bs_sem.at[c], br_sem.at[c], "tm", down)
+
+    for c in range(PIECES):
 
         @pl.when(has_up)
         def _():
             b_copy(c).wait_recv()
 
-        dnew = dz[chunk[c]] + cot_ref[chunk[c]]
-        pre = dnew * coef_a[chunk[c]]
-        gate = dnew * coef_b[chunk[c]]
+        dnew = dz[piece[c]] + cot_ref[piece[c]]
+        pre = dnew * coef_a[piece[c]]
+        gate = dnew * coef_b[piece[c]]
         pre_pieces = split(pre)
-        dagg[chunk[c]] = dot3(pre_pieces, both(wn), NT)
+        dagg[piece[c]] = dot3(pre_pieces, both(wn), NT)
 
         @pl.when(has_down)
         def _():
             for off in range(1, n_ent):
                 g_copy(off, c).start()
 
-        dpre[chunk[c]] = pre
-        dgate[chunk[c]] = gate
+        dpre[piece[c]] = pre
+        dgate[piece[c]] = gate
 
         @pl.when(has_down)
         def _():
-            dprev[chunk[c]] = (
-                dnew * (1.0 - upd[chunk[c]])
+            dprev[piece[c]] = (
+                dnew * (1.0 - upd[piece[c]])
                 + dot3(pre_pieces, both(ws), NT)
                 + dot3(split(gate), both(wg), NT)
             )
@@ -234,7 +239,8 @@
             own = dagg[chunk[c]]
             spread = [own * hits[0][k] for k in range(n_tile)]
             for off in range(1, n_ent):
-                g_copy(off, c).wait_recv()
+                for p in inside[c]:
+                    g_copy(off, p).wait_recv()
                 other = grecv[off - 1, chunk[c]]
                 for k in range(n_tile):
                     spread[k] = spread[k] + other * hits[n_ent - off][k]
@@ -245,9 +251,9 @@
                     for k in range(n_tile)
                 )
             else:
-                for d in range(CHUNKS):
-                    dout[chunk[d]] = dprev[chunk[d]] + sum(
-                        dot3(both((tth, ttl), k, chunk[d], chunk[c]), pieces[k])
+                for d in range(PIECES):
+                    dout[piece[d]] = dprev[piece[d]] + sum(
+                        dot3(both((tth, ttl), k, piece[d], chunk[c]), pieces[k])
                         for k in range(n_tile)
                     )
                     b_copy(d).start()
@@ -372,17 +378,17 @@
 
     for off in range(1, n_ent):
         m_copy(off).wait_send()
-        for c in range(CHUNKS):
+        for c in range(PIECES):
             y_copy(off, c).wait_send()
 
     @pl.when(has_up)
     def _():
-        for c in range(CHUNKS):
+        for c in range(PIECES):
             z_copy(c).wait_send()
 
     @pl.when(has_down)
     def _():
-        for c in range(CHUNKS):
+        for c in range(PIECES):
             b_copy(c).wait_send()
             for off in range(1, n_ent):
                 g_copy(off, c).wait_send()
@@ -432,10 +438,10 @@
             vmem((members * size, width), f32), vmem((mates, size, width), f32),
             vmem((size, width), f32), vmem((size, width), f32),
             vmem((shards * size, width), f32),
-            sems((others, CHUNKS)), sems((others, CHUNKS)),
-            sems((others, CHUNKS)), sems((others, CHUNKS)),
+            sems((others, PIECES)), sems((others, PIECES)),
+            sems((others, PIECES)), sems((others, PIECES)),
             sems((others,)), sems((others,)),
-            sems((CHUNKS,)), sems((CHUNKS,)), sems((CHUNKS,)), sems((CHUNKS,)),
+            sems((PIECES,)), sems((PIECES,)), sems((PIECES,)), sems((PIECES,)),
             sems((7,)), sems((mates,)), sems((mates,)), sems((n_tm,)),
             sems((mates,)), sems((mates,)),
         ],

time: 158 us -> 153 us (0.968)
  Pallas kernels: 150 us -> 144 us
    pallas_call x1, Pallas kernels: 150 us -> 144 us  [on_device(): pl.pallas_call(functools.partial(step_kernel, n_tm, n_ent, n_batch), out_...]
where the time goes in v3:
time: 153 us; the launch traced here: 152 us
  Pallas kernels  144 us (94%)
  local copies, waits for them, and re-layouts  7.24 us (5%)
    pallas_call x1, Pallas kernels, on_device(): pl.pallas_call(functools.partial(step_kernel, n_tm, n_ent, n_batch), out_...  144 us
    unnamed x12, local copies, waits for them, and re-layouts  7.24 us

profile of v3, /device:TPU:13, one launch (start us, length us, event | category | flops | bytes accessed | tf_op | source)
XLA Modules:
  0.0 152.3 jit_solution(11723738335109074897)
XLA Ops:
  0.6 144.4 %shard_map.145 = (f32[512,256]{1,0:T(8,128)}, f32[256,256]{1,0:T(8,128)}, f32[256,256]{1,0:T(8,128)}, f32[256,256]{1,0:T(8,128)}, f32[256,256]{1,0:T(8,128)}, /*index=5*/f32[1,256]{1,0:T(1,128)}) custom-call(s32[2]{0:T(128)} %bitcast.14, s32[2]{0:T(128)} %bitcast.15, f32[512,256]{1,0:T(8,128)} %bitcast.10, f32[2,512,512]{2,1,0:T(8,128)} %bitcast.8, ...), custom_call_target="tpu_custom_call" | custom-call | tf_op jit(solution)/shard_map/pallas_call | solution.py:416
  145.0 0.0 copy-start.1
  145.0 0.0 copy-start
  145.0 0.0 copy-start.2
  145.0 1.9 %copy.22 = f32[1,1,512,256]{3,2,1,0:T(8,128)} copy(f32[1,1,512,256]{3,2,1,0:T(8,128)} %bitcast.9) | data formatting | bytes 1048576
  146.9 1.7 %copy.23 = f32[256,256]{1,0:T(8,128)} copy(f32[256,256]{1,0:T(8,128)} %get-tuple-element.25) | data formatting | bytes 524288
  148.6 1.7 %copy.24 = f32[256,256]{1,0:T(8,128)} copy(f32[256,256]{1,0:T(8,128)} %get-tuple-element.26) | data formatting | bytes 524288
  150.3 0.0 copy-done.1
  150.3 0.7 copy.25
  151.0 0.0 copy-done
  151.0 0.7 copy.26
  151.7 0.0 copy-done.2
  151.7 0.6 copy.27
Async XLA Ops:
  145.0 5.3 %copy-start.1 = (f32[256,256]{1,0:T(8,128)S(1)}, f32[256,256]{1,0:T(8,128)}, u32[]{:S(2)}) copy-start(f32[256,256]{1,0:T(8,128)} %get-tuple-element.27) | copy-start | bytes 786436
  145.0 6.0 %copy-start = (f32[256,256]{1,0:T(8,128)S(1)}, f32[256,256]{1,0:T(8,128)}, u32[]{:S(2)}) copy-start(f32[256,256]{1,0:T(8,128)} %get-tuple-element.28) | copy-start | bytes 786436
  145.0 6.7 %copy-start.2 = (f32[1,256]{1,0:T(1,128)S(1)}, f32[1,256]{1,0:T(1,128)}, u32[]{:S(2)}) copy-start(f32[1,256]{1,0:T(1,128)} %get-tuple-element.17) | copy-start | bytes 3076
